TPU v7x, 32 devices: a whole 2x2x4 slice. The times are simulated.
32 devices in a mesh: grp: 2 (over x), lat: 16 (over z, y, core).
Axes of the slice: x: 2, y: 2, z: 4, core: 2. Of those that a mesh axis runs over, the one named last changes fastest.
Arguments:
- acts: bfloat16 [128, 2, 2048], P(('grp', 'lat')), parts along dimension 0, may hold values from -6 to 6
- enc_weight: bfloat16 [4, 2048, 4096], P('grp', None, 'lat'), parts along dimension 0, may hold values from -0.09375 to 0.09375
- enc_bias: float32 [8192], P(('grp', 'lat')), parts along dimension 0, may hold values from -3 to 3
- dec_weight: bfloat16 [4096, 4, 2048], P('lat', 'grp'), parts along dimension 1, may hold values from -0.125 to 0.125
- dec_bias: float32 [4, 2048], P('grp'), parts along dimension 0, may hold values from -5 to 5
Outputs:
- residual: bfloat16 [128, 2, 2048], P(('grp', 'lat')), parts along dimension 0
- grad_enc: bfloat16 [4, 2048, 4096], P('grp', None, 'lat'), parts along dimension 0
- grad_enc_bias: float32 [8192], P(('grp', 'lat')), parts along dimension 0
- grad_dec: bfloat16 [4096, 4, 2048], P('lat', 'grp'), parts along dimension 1
- grad_dec_bias: float32 [4, 2048], P('grp'), parts along dimension 0
There are 2 independent parts, one for each index of `grp`. A program takes and returns all parts, laid end to end along the dimension named above; each array names one. Nothing has to cross between parts.
All inputs are finite; a program needn't handle non-finite values.
Results may differ from a plain program's by a relative error of at most 0.015.
Values may be sent and summed in bfloat16 or wider, within the bound.
A program may use at most 128 MiB of HBM per device.

v0:
```python
import jax
import jax.numpy as jnp
from jax import lax
from jax.sharding import PartitionSpec as P

sparsity_weight = 2.0


def body(acts, enc_weight, enc_bias, dec_weight, dec_bias):
    tok_dev, layers, width = acts.shape
    lat_dev = enc_weight.shape[2]
    wide = layers * width
    total_rows = tok_dev * lax.axis_size("lat")
    factor = 2.0 / total_rows
    flat_rows = acts.reshape(tok_dev, wide)
    flat_enc = enc_weight.reshape(wide, lat_dev)
    flat_dec = dec_weight.reshape(lat_dev, wide)
    flat_bias = dec_bias.reshape(wide)
    own_start = lax.axis_index("lat") * tok_dev
    gathered = lax.all_gather(flat_rows, "lat", axis=0, tiled=True)
    before = jnp.dot(gathered, flat_enc, preferred_element_type=jnp.float32) + enc_bias
    active = jnp.maximum(before, 0.0).astype(jnp.bfloat16)
    dec_wide = dec_weight.astype(jnp.float32)
    row_sq = jnp.sum(dec_wide * dec_wide, axis=2)
    inv_norm = lax.rsqrt(row_sq + 1.0)
    dec_norm = jnp.sum(jnp.sqrt(row_sq + 1.0), axis=1)
    term = jnp.dot(active, flat_dec, preferred_element_type=jnp.float32)
    own_term = lax.dynamic_slice_in_dim(term, own_start, tok_dev, 0)
    own_term = own_term + flat_bias - flat_rows.astype(jnp.float32)
    term = lax.dynamic_update_slice_in_dim(term, own_term, own_start, 0)
    summed = lax.psum(term, "lat")
    all_residual = summed.astype(jnp.bfloat16)
    own_residual = lax.dynamic_slice_in_dim(all_residual, own_start, tok_dev, 0)
    grad_dec_bias = factor * jnp.sum(all_residual.astype(jnp.float32), axis=0)
    dec_total = lax.dot_general(
        active, all_residual, (((0,), (0,)), ((), ())), preferred_element_type=jnp.float32
    )
    backward = lax.dot_general(
        all_residual, flat_dec, (((1,), (1,)), ((), ())), preferred_element_type=jnp.float32
    )
    grad_act = factor * backward + sparsity_weight / total_rows * dec_norm
    grad_before = jnp.where(before > 0.0, grad_act, 0.0).astype(jnp.bfloat16)
    enc_total = lax.dot_general(
        gathered, grad_before, (((0,), (0,)), ((), ())), preferred_element_type=jnp.float32
    )
    grad_enc = enc_total.astype(jnp.bfloat16).reshape(layers, width, lat_dev)
    grad_enc_bias = jnp.sum(grad_before.astype(jnp.float32), axis=0)
    act_sum = jnp.sum(active.astype(jnp.float32), axis=0)
    grad_dec = (
        factor * dec_total.reshape(lat_dev, layers, width)
        + sparsity_weight / total_rows * act_sum[:, None, None] * dec_wide * inv_norm[:, :, None]
    ).astype(jnp.bfloat16)
    return (
        own_residual.reshape(tok_dev, layers, width),
        grad_enc,
        grad_enc_bias,
        grad_dec,
        grad_dec_bias.reshape(layers, width),
    )


def solution(mesh):
    return jax.shard_map(
        body,
        mesh=mesh,
        in_specs=(
            P(("grp", "lat"), None, None),
            P("grp", None, "lat"),
            P(("grp", "lat")),
            P("lat", "grp", None),
            P("grp", None),
        ),
        out_specs=(
            P(("grp", "lat"), None, None),
            P("grp", None, "lat"),
            P(("grp", "lat")),
            P("lat", "grp", None),
            P("grp", None),
        ),
        check_vma=False,
    )
```

profile of v0, /device:TPU:0, one launch (start us, length us, event | category | flops | bytes accessed | tf_op | source)
XLA Modules:
  0.0 136.5 jit_solution(2590079693091624209)
XLA Ops:
  0.6 0.0 copy-start
  0.7 1.6 %copy-done = bf16[2,2048,256]{2,1,0:T(8,128)(2,1)S(1)} copy-done((bf16[2,2048,256]{2,1,0:T(8,128)(2,1)S(1)}, bf16[2,2048,256]{2,1,0:T(8,128)(2,1)}, u32[]{:S(2)}) %copy-start) | copy-done | bytes 2097176
  2.2 0.7 copy.14
  2.9 0.8 reshape.50
  3.7 0.8 convert_bitcast_fusion
  4.5 0.0 copy-start.3
  4.6 3.8 %fusion.1 = f32[256,2]{1,0:T(8,128)S(1)} fusion(bf16[256,2,2048]{2,1,0:T(2,128)(2,1)} %param.8), kind=kLoop, calls=%fused_computation.5 | loop fusion | flops 3145216 | bytes 2099200 | tf_op jit(solution)/shard_map/reduce_sum | solution.py:24
  8.4 0.1 add_rsqrt_fusion
  8.6 24.6 %all-gather = bf16[16,4,4096]{2,1,0:T(4,128)(2,1)S(1)} all-gather(bf16[1,4,4096]{2,1,0:T(4,128)(2,1)S(1)} %reshape.50), channel_id=1, replica_groups=mesh['grp'=2,'lat'=16] {'lat'}, dimensions={0}, use_global_device_ids=true | all-gather | bytes 557056 | tf_op jit(solution)/shard_map/all_gather | solution.py:20
  33.2 0.1 reshape.51
  33.3 0.0 copy-done.3
  33.3 0.0 copy-start.1
  33.3 0.5 convert_reduce_fusion.1
  33.8 1.1 copy-done.1
  34.9 0.9 copy.13
  35.8 0.0 copy-start.2
  35.8 1.3 copy-done.2
  37.1 1.5 %fusion.8 = f32[64,4096]{1,0:T(8,128)} fusion(bf16[256,4096]{1,0:T(8,128)(2,1)S(1)} %bitcast.21, f32[64,256]{1,0:T(8,128)S(1)} %get-tuple-element.20), kind=kOutput, calls=%fused_computation.26 | convolution fusion | flops 134250496 | bytes 3211264 | tf_op jit(solution)/shard_map/dot_general | solution.py:27
  38.6 1.6 %subtract_dynamic-update-slice_fusion = f32[64,4096]{1,0:T(8,128)} fusion(f32[64,4096]{1,0:T(8,128)} %fusion.8, s32[]{:T(128)S(6)} %select_n.9, f32[4,4096]{1,0:T(4,128)S(1)} %bitcast.24, f32[4096]{0:T(1024)S(1)} %bitcast.25), kind=kLoop, calls=%fused_computation.20 | loop fusion | flops 32768 | bytes 212996 | tf_op jit(solution)/shard_map/dynamic_update_slice | solution.py:30
  40.1 70.1 %all-reduce.1 = bf16[64,4096]{1,0:T(8,128)(2,1)S(1)} all-reduce(f32[64,4096]{1,0:T(8,128)} %subtract_dynamic-update-slice_fusion), channel_id=1, replica_groups=mesh['grp'=2,'lat'=16] {'lat'}, use_global_device_ids=true, to_apply=%region_0.0 | all-reduce | flops 262144 | bytes 1572864 | tf_op jit(solution)/shard_map/psum | solution.py:31
  110.2 2.9 %convert_reduce_fusion.2 = (f32[256]{0:T(256)}, bf16[64,256]{1,0:T(8,128)(2,1)S(1)}) fusion(f32[256]{0:T(256)S(1)} %broadcast_multiply_fusion.2, bf16[64,4096]{1,0:T(8,128)(2,1)S(1)} %all-reduce.1, bf16[256,4096]{1,0:T(8,128)(2,1)} %bitcast.22, f32[64,256]{1,0:T(8,128)S(1)} %get-tuple-element.20), kind=kOutput, calls=%fused_computation.19 | convolution fusion | flops 134332160 | bytes 2721792 | tf_op jit(solution)/shard_map/dot_general | solution.py:38
  113.1 0.1 convert_reduce_fusion
  113.3 0.6 mul.82
  113.9 0.7 reshape.48
  114.6 2.0 %fusion = bf16[4096,256]{0,1:T(8,128)(2,1)} fusion(bf16[64,256]{1,0:T(8,128)(2,1)S(1)} %get-tuple-element.18, bf16[64,4096]{1,0:T(8,128)(2,1)S(1)} %reshape.51), kind=kOutput, calls=%fused_computation.4 | convolution fusion | flops 135266304 | bytes 2654208 | tf_op jit(solution)/shard_map/dot_general | solution.py:43
  116.6 4.1 %copy.12 = bf16[4096,256]{1,0:T(8,128)(2,1)} copy(bf16[4096,256]{0,1:T(8,128)(2,1)} %fusion) | data formatting | bytes 4194304
  120.7 2.7 %convolution_multiply_fusion = f32[256,4096]{1,0:T(8,128)} fusion(bf16[64,4096]{1,0:T(8,128)(2,1)S(1)} %all-reduce.1, f32[64,256]{1,0:T(8,128)S(1)} %get-tuple-element.20), kind=kOutput, calls=%fused_computation | convolution fusion | flops 135299072 | bytes 4784128 | tf_op jit(solution)/shard_map/dot_general | solution.py:35
  123.3 6.6 %mul.74 = f32[256,2,2048]{2,1,0:T(2,128)} reshape(f32[256,4096]{1,0:T(8,128)} %convolution_multiply_fusion) | data formatting | bytes 8388608 | tf_op jit(solution)/shard_map/mul | solution.py:50
  129.9 6.7 %fusion.4 = bf16[256,2,2048]{2,1,0:T(2,128)(2,1)} fusion(f32[256,2,2048]{2,1,0:T(2,128)} %mul.74, bf16[256,2,2048]{2,1,0:T(2,128)(2,1)} %param.8, f32[256]{0:T(256)S(1)} %broadcast_multiply_fusion.1, f32[256,2]{1,0:T(8,128)S(1)} %get-tuple-element.15), kind=kLoop, calls=%fused_computation.8 | loop fusion | flops 5242880 | bytes 8391680 | tf_op jit(solution)/shard_map/convert_element_type | solution.py:52
  (5 shorter events, 0.1 us)
Async XLA Ops:
  0.6 1.6 %copy-start = (bf16[2,2048,256]{2,1,0:T(8,128)(2,1)S(1)}, bf16[2,2048,256]{2,1,0:T(8,128)(2,1)}, u32[]{:S(2)}) copy-start(bf16[2,2048,256]{2,1,0:T(8,128)(2,1)} %param.6) | copy-start | bytes 6291460
  4.5 28.8 %copy-start.3 = (f32[256]{0:T(256)S(1)}, f32[256]{0:T(256)}, u32[]{:S(2)}) copy-start(f32[256]{0:T(256)} %param.7) | copy-start | bytes 3076
  33.3 1.6 %copy-start.1 = (bf16[256,2,2048]{2,1,0:T(2,128)(2,1)S(1)}, bf16[256,2,2048]{2,1,0:T(2,128)(2,1)}, u32[]{:S(2)}) copy-start(bf16[256,2,2048]{2,1,0:T(2,128)(2,1)} %param.8) | copy-start | bytes 6291460
  35.8 1.3 copy-start.2
where the time goes:
time: 137 us
  blocking collectives  94.7 us (69%)
  local copies, waits for them, and re-layouts  18.5 us (14%)
  other arithmetic  13.1 us (10%)
  matrix products  9.56 us (7%)
    psum x1, blocking collectives, body(): summed = lax.psum(term, 'lat')  70.1 us
    all_gather x1, blocking collectives, body(): gathered = lax.all_gather(flat_rows, 'lat', axis=0, tiled=True)  24.6 us
    unnamed x14, local copies, waits for them, and re-layouts  10.6 us
    convert_element_type x1, other arithmetic, body(): grad_dec = (factor * dec_total.reshape(lat_dev, layers, width) + sparsity...  6.65 us
    mul x1, local copies, waits for them, and re-layouts, body(): factor * dec_total.reshape(lat_dev, layers, width)  6.57 us
    reduce_sum x1, other arithmetic, body(): row_sq = jnp.sum(dec_wide * dec_wide, axis=2)  3.84 us
    dot_general x1, matrix products, body(): lax.dot_general(all_residual, flat_dec, (((1,), (1,)), ((), ())), preferr...  2.94 us

commit v1 on v0

v1 whole, which is shorter than its diff:
```python
import functools

import jax
import jax.numpy as jnp
from jax import lax
from jax.experimental import pallas as pl
from jax.experimental.pallas import tpu as pltpu
from jax.sharding import PartitionSpec as P

sparsity_weight = 2.0
f32, bf16 = jnp.float32, jnp.bfloat16


def dot(a, b, ca=1, cb=0):
    return lax.dot_general(a, b, (((ca,), (cb,)), ((), ())), preferred_element_type=f32)


def pair_expander(lat_dev, layers):
    row = lax.broadcasted_iota(jnp.int32, (lat_dev, lat_dev * layers), 0)
    col = lax.broadcasted_iota(jnp.int32, (lat_dev, lat_dev * layers), 1)
    return jnp.where(col // layers == row, 1.0, 0.0).astype(bf16)


def layer_major(rows, layers):
    size = rows * layers
    row = lax.broadcasted_iota(jnp.int32, (size, size), 0)
    col = lax.broadcasted_iota(jnp.int32, (size, size), 1)
    return jnp.where(row % rows * layers + row // rows == col, 1.0, 0.0).astype(bf16)


def spread_active(active, layers):
    rows, lat_dev = active.shape
    wide = dot(active, pair_expander(lat_dev, layers))
    layer = lax.broadcasted_iota(jnp.int32, wide.shape, 1) % layers
    parts = [jnp.where(layer == l, wide, 0.0).astype(bf16) for l in range(layers)]
    return jnp.concatenate(parts, axis=0)


def gather_kernel_body(n, src, buf, own_block, sems, me, send_to):
    chips = n // 2
    chip, core = me // 2, me % 2
    partner = me + 1 - 2 * core
    send, recv, fsend, frecv = sems

    def put(src_ref, index, ssem, rsem, dev):
        return pltpu.make_async_remote_copy(
            src_ref=src_ref, dst_ref=buf.at[index], send_sem=ssem, recv_sem=rsem,
            device_id={"lat": dev}, device_id_type=pl.DeviceIdType.MESH)

    first = []
    for q in range(1, chips):
        dev = lax.rem(chip + q, chips) * 2 + core
        c = put(src, me, send.at[q], recv.at[q], dev)
        c.start()
        first.append(c)
    second = [put(src, me, fsend.at[0], frecv.at[0], partner)]
    second[0].start()
    own_block()
    for q in range(1, chips):
        first[q - 1].wait_recv()
        origin = lax.rem(chip - q + chips, chips) * 2 + core
        c = put(buf.at[origin], origin, fsend.at[q], frecv.at[q], partner)
        c.start()
        second.append(c)
    for c in second:
        c.wait_recv()
    return first + second


def forward_kernel(n, acts, enc_hbm, bias, dec_hbm, dbias,
                   xl_out, rl_out, own_out, before_out, inv_out, norm_out,
                   enc, dec, w2, xbuf, rbuf, wide, rsrc, pair_out, pair_in, sum_out, sum_in,
                   local_sem, ag_sem, rg_sem, pair_sem, sum_sem):
    me = lax.axis_index("lat")
    chips = n // 2
    chip, core = me // 2, me % 2
    partner = me + 1 - 2 * core
    tok_dev, layers, width = acts.shape
    lat_dev = dec.shape[0]
    rows = n * tok_dev
    block = tok_dev * layers

    enc_copy = pltpu.make_async_copy(enc_hbm, enc, local_sem.at[0])
    dec_copy = pltpu.make_async_copy(dec_hbm, dec, local_sem.at[1])
    enc_copy.start()
    dec_copy.start()
    barrier = pltpu.get_barrier_semaphore()
    for q in range(1, chips):
        dev = lax.rem(chip + q, chips) * 2 + core
        pl.semaphore_signal(barrier, inc=1, device_id={"lat": dev}, device_id_type=pl.DeviceIdType.MESH)
    pl.semaphore_signal(barrier, inc=1, device_id={"lat": partner}, device_id_type=pl.DeviceIdType.MESH)
    pl.semaphore_wait(barrier, chips)

    def weight_work():
        xbuf[me] = acts[...]
        dec_copy.wait()
        square = jnp.zeros((lat_dev * layers, 128), f32)
        for c in range(0, width, 512):
            piece = dec[:, :, c:c + 512].reshape(lat_dev * layers, 512)
            w2[:, c:c + 512] = piece
            p = piece.astype(f32)
            p = p * p
            for k in range(4):
                square = square + p[:, k * 128:(k + 1) * 128]
        total = jnp.sum(square, axis=1, keepdims=True) + 1.0
        inv_out[...] = lax.rsqrt(total)
        norm = jnp.broadcast_to(jnp.sqrt(total), (lat_dev * layers, 128))
        norm_out[...] = jnp.transpose(norm)[:8, :]
        enc_copy.wait()

    started = gather_kernel_body(n, acts, xbuf, weight_work, [ag_sem.at[i] for i in range(4)], me, None)

    order_rows = layer_major(rows, layers)
    before = bias[...].reshape(1, lat_dev)
    for c in range(0, width, 512):
        piece = dot(order_rows, xbuf[:, :, :, c:c + 512].reshape(rows * layers, 512)).astype(bf16)
        xl_out[:, c:c + 512] = piece
        for l in range(layers):
            before = before + dot(piece[l * rows:(l + 1) * rows, :], enc[l, c:c + 512, :])
    before_out[...] = before
    active = jnp.maximum(before, 0.0).astype(bf16)
    spread = dot(order_rows, spread_active(active, layers), 0, 0).astype(bf16)
    for c in range(0, width, 512):
        wide[:, c:c + 512] = dot(spread, w2[:, c:c + 512])

    def chunk(dev):
        return wide[pl.ds(pl.multiple_of(dev * block, block), block), :]

    order = list(range(1, chips)) + [0]
    pairs = {}
    for q in order:
        k = lax.rem(chip + q, chips)
        pair_out[q] = chunk(k * 2 + 1 - core).astype(bf16)
        c = pltpu.make_async_remote_copy(
            src_ref=pair_out.at[q], dst_ref=pair_in.at[q], send_sem=pair_sem.at[0, q], recv_sem=pair_sem.at[1, q],
            device_id={"lat": partner}, device_id_type=pl.DeviceIdType.MESH)
        c.start()
        pairs[q] = c
    sums = []
    for q in order:
        k = lax.rem(chip + q, chips)
        pairs[q].wait_recv()
        both = chunk(k * 2 + core) + pair_in[q].astype(f32)
        if q == 0:
            total = both
        else:
            sum_out[q] = both.astype(bf16)
            c = pltpu.make_async_remote_copy(
                src_ref=sum_out.at[q], dst_ref=sum_in.at[q], send_sem=sum_sem.at[0, q], recv_sem=sum_sem.at[1, q],
                device_id={"lat": k * 2 + core}, device_id_type=pl.DeviceIdType.MESH)
            c.start()
            sums.append(c)
    layer = lax.broadcasted_iota(jnp.int32, (block, width), 0) % layers
    shift = jnp.zeros((block, width), f32)
    for l in range(layers):
        shift = jnp.where(layer == l, dbias[l:l + 1, :], shift)
    total = total + shift - acts[...].reshape(block, width).astype(f32)
    for q in range(1, chips):
        sums[q - 1].wait_recv()
        total = total + sum_in[q].astype(f32)
    residual = total.astype(bf16)
    rsrc[...] = residual
    own_out[...] = residual

    def own_residual():
        rbuf[me] = residual

    started += gather_kernel_body(n, rsrc, rbuf, own_residual, [rg_sem.at[i] for i in range(4)], me, None)
    for c in range(0, width, 512):
        piece = rbuf[:, :, c:c + 512].astype(f32).reshape(rows * layers, 512).astype(bf16)
        rl_out[:, c:c + 512] = dot(order_rows, piece).astype(bf16)
    for c in started + list(pairs.values()) + sums:
        c.wait_send()


def backward_kernel(xl, rl, own, before, inv, norm, dec, residual, genc, gencb, gdec, gdecb):
    layers, width, lat_dev = genc.shape
    rows = before.shape[0]
    factor = 2.0 / rows
    step = 512
    residual[...] = own[...].reshape(residual.shape)
    back = jnp.zeros((rows * layers, lat_dev * layers), f32)
    for c in range(0, width, step):
        back = back + dot(rl[:, c:c + step], dec[:, :, c:c + step].reshape(lat_dev * layers, step), 1, 1)
    layer = lax.broadcasted_iota(jnp.int32, (rows, lat_dev * layers), 1) % layers
    value = jnp.zeros((rows, lat_dev * layers), f32)
    for l in range(layers):
        value = jnp.where(layer == l, back[l * rows:(l + 1) * rows, :], value)
    value = factor * value + (sparsity_weight / rows) * norm[0:1, :]
    high = value.astype(bf16)
    low = (value - high.astype(f32)).astype(bf16)
    expand = pair_expander(lat_dev, layers)
    grad_act = dot(high, expand, 1, 1) + dot(low, expand, 1, 1)
    pre = before[...]
    grad_before = jnp.where(pre > 0.0, grad_act, 0.0).astype(bf16)
    gencb[...] = jnp.sum(grad_before.astype(f32), axis=0, keepdims=True)
    for l in range(layers):
        for c in range(0, width, step):
            genc[l, c:c + step, :] = dot(xl[l * rows:(l + 1) * rows, c:c + step], grad_before, 0, 0).astype(bf16)
    spread = spread_active(jnp.maximum(pre, 0.0).astype(bf16), layers)
    act_sum = dot(spread, jnp.ones((rows * layers, 128), bf16), 0, 0)[:, :1]
    scale = (sparsity_weight / rows) * act_sum * inv[...]
    for c in range(0, width, step):
        wide = dec[:, :, c:c + step].reshape(lat_dev * layers, step).astype(f32)
        out = factor * dot(spread, rl[:, c:c + step], 0, 0) + scale * wide
        gdec[:, :, c:c + step] = out.astype(bf16).reshape(lat_dev, layers, step)
    for l in range(layers):
        gdecb[l:l + 1, :] = factor * jnp.sum(rl[l * rows:(l + 1) * rows, :].astype(f32), axis=0, keepdims=True)


def body(n, acts, enc_weight, enc_bias, dec_weight, dec_bias):
    tok_dev, layers, width = acts.shape
    lat_dev = enc_weight.shape[2]
    rows, block, chips = n * tok_dev, tok_dev * layers, n // 2
    vmem = pl.BlockSpec(memory_space=pltpu.VMEM)
    hbm = pl.BlockSpec(memory_space=pl.ANY)
    shape = jax.ShapeDtypeStruct
    dma = pltpu.SemaphoreType.DMA
    xl, rl, own, before, inv, norm = pl.pallas_call(
        functools.partial(forward_kernel, n),
        out_shape=(
            shape((rows * layers, width), bf16),
            shape((rows * layers, width), bf16),
            shape((block, width), bf16),
            shape((rows, lat_dev), f32),
            shape((lat_dev * layers, 1), f32),
            shape((8, lat_dev * layers), f32),
        ),
        in_specs=[vmem, hbm, vmem, hbm, vmem],
        out_specs=(vmem,) * 6,
        scratch_shapes=[
            pltpu.VMEM(enc_weight.shape, bf16),
            pltpu.VMEM(dec_weight.shape, bf16),
            pltpu.VMEM((lat_dev * layers, width), bf16),
            pltpu.VMEM((n, tok_dev, layers, width), bf16),
            pltpu.VMEM((n, block, width), bf16),
            pltpu.VMEM((rows * layers, width), f32),
            pltpu.VMEM((block, width), bf16),
            pltpu.VMEM((chips, block, width), bf16),
            pltpu.VMEM((chips, block, width), bf16),
            pltpu.VMEM((chips, block, width), bf16),
            pltpu.VMEM((chips, block, width), bf16),
            dma((2,)),
            dma((4, chips)),
            dma((4, chips)),
            dma((2, chips)),
            dma((2, chips)),
        ],
        compiler_params=pltpu.CompilerParams(
            collective_id=0, has_side_effects=True, vmem_limit_bytes=56 * 1024 * 1024),
        name="forward",
    )(acts, enc_weight, enc_bias.reshape(1, lat_dev), dec_weight, dec_bias)
    residual, genc, gencb, gdec, gdecb = pl.pallas_call(
        backward_kernel,
        out_shape=(
            shape(acts.shape, bf16),
            shape(enc_weight.shape, bf16),
            shape((1, lat_dev), f32),
            shape(dec_weight.shape, bf16),
            shape(dec_bias.shape, f32),
        ),
        in_specs=[vmem] * 7,
        out_specs=(vmem,) * 5,
        compiler_params=pltpu.CompilerParams(vmem_limit_bytes=56 * 1024 * 1024),
        name="backward",
    )(xl, rl, own, before, inv, norm, dec_weight)
    return residual, genc, gencb.reshape(lat_dev), gdec, gdecb


def solution(mesh):
    specs = (
        P(("grp", "lat"), None, None),
        P("grp", None, "lat"),
        P(("grp", "lat")),
        P("lat", "grp", None),
        P("grp", None),
    )
    return jax.shard_map(
        functools.partial(body, mesh.shape["lat"]),
        mesh=mesh, in_specs=specs, out_specs=specs, check_vma=False,
    )
```

time: 137 us -> 42.3 us (0.31)
  blocking collectives: 94.7 us -> 0 us
  Pallas kernels: 0 us -> 41.2 us
  local copies, waits for them, and re-layouts: 18.5 us -> 0 us
  other arithmetic: 13.1 us -> 0 us
  matrix products: 9.56 us -> 0 us
    psum x1 -> x0, blocking collectives: 70.1 us -> none  [body(): summed = lax.psum(term, 'lat')]
    pallas_call x0 -> x2, Pallas kernels: none -> 41.2 us  [the longest x1 34.2 us: body(): pl.pallas_call(functools.partial(forward_kernel, n), out_shape=(shape((ro...]
    all_gather x1 -> x0, blocking collectives: 24.6 us -> none  [body(): gathered = lax.all_gather(flat_rows, 'lat', axis=0, tiled=True)]
    unnamed x14 -> x0, local copies, waits for them, and re-layouts: 10.6 us -> none
    dot_general x5 -> x0, matrix products: 9.56 us -> none  [the longest x1 2.94 us: body(): lax.dot_general(all_residual, flat_dec, (((1,), (1,)), ((), ())), preferr...]
    mul x2 -> x0, local copies, waits for them, and re-layouts: 7.19 us -> none  [the longest x1 6.57 us: body(): factor * dec_total.reshape(lat_dev, layers, width)]
    convert_element_type x1 -> x0, other arithmetic: 6.65 us -> none  [body(): grad_dec = (factor * dec_total.reshape(lat_dev, layers, width) + sparsity...]
    reduce_sum x2 -> x0, other arithmetic: 3.94 us -> none  [the longest x1 3.84 us: body(): row_sq = jnp.sum(dec_wide * dec_wide, axis=2)]
where the time goes in v1:
time: 42.3 us; the launch traced here: 41.8 us
  Pallas kernels  41.2 us (97%)
  between operations  0.64 us (2%)
    pallas_call x1, Pallas kernels, body(): pl.pallas_call(functools.partial(forward_kernel, n), out_shape=(shape((ro...  34.2 us
    pallas_call x1, Pallas kernels, body(): pl.pallas_call(backward_kernel, out_shape=(shape(acts.shape, bf16), shape...  7 us

profile of v1, /device:TPU:0, one launch (start us, length us, event | category | flops | bytes accessed | tf_op | source)
XLA Modules:
  0.0 41.8 jit_solution(13280719688578886026)
XLA Ops:
  0.6 34.2 %forward.1 = (bf16[128,2048]{1,0:T(8,128)(2,1)}, bf16[128,2048]{1,0:T(8,128)(2,1)}, bf16[8,2048]{1,0:T(8,128)(2,1)}, f32[64,256]{1,0:T(8,128)}, f32[512,1]{1,0:T(8,128)}, /*index=5*/f32[8,512]{1,0:T(8,128)}) custom-call(bf16[4,2,2048]{2,1,0:T(2,128)(2,1)} %acts.1, bf16[2,2048,256]{2,1,0:T(8,128)(2,1)} %enc_hbm.1, f32[1,256]{1,0:T(1,128)} %bitcast.2, ...), custom_call_target="tpu_custom_call" | custom-call | tf_op jit(solution)/shard_map/forward/pallas_call | solution.py:219
  34.8 7.0 %backward.1 = (bf16[4,2,2048]{2,1,0:T(2,128)(2,1)}, bf16[2,2048,256]{2,1,0:T(8,128)(2,1)}, f32[1,256]{1,0:T(1,128)}, bf16[256,2,2048]{2,1,0:T(2,128)(2,1)}, f32[2,2048]{1,0:T(2,128)}) custom-call(bf16[128,2048]{1,0:T(8,128)(2,1)} %get-tuple-element.16.xl, bf16[128,2048]{1,0:T(8,128)(2,1)} %get-tuple-element.17.rl, bf16[8,2048]{1,0:T(8,128)(2,1)} %get-tuple-element.18.own, ...), custom_call_target="tpu_custom_call" | custom-call | tf_op jit(solution)/shard_map/backward/pallas_call | solution.py:253

commit v2 on v1

--- a/solution.py
+++ b/solution.py
@@ -36,41 +36,58 @@
     return jnp.concatenate(parts, axis=0)
 
 
-def gather_kernel_body(n, src, buf, own_block, sems, me, send_to):
+def grid_of(n):
     chips = n // 2
-    chip, core = me // 2, me % 2
+    inner = max(k for k in range(1, chips + 1) if chips % k == 0 and k * k <= chips)
+    return chips // inner, inner
+
+
+def gather_blocks(n, src, buf, own_block, outer_sem, inner_sem, core_sem):
+    outer, inner = grid_of(n)
+    me = lax.axis_index("lat")
+    core, y, z = me % 2, me // 2 % inner, me // (2 * inner)
     partner = me + 1 - 2 * core
-    send, recv, fsend, frecv = sems
-
-    def put(src_ref, index, ssem, rsem, dev):
-        return pltpu.make_async_remote_copy(
-            src_ref=src_ref, dst_ref=buf.at[index], send_sem=ssem, recv_sem=rsem,
+    started = []
+
+    def put(src_ref, index, sems, slot, dev):
+        c = pltpu.make_async_remote_copy(
+            src_ref=src_ref, dst_ref=buf.at[index],
+            send_sem=sems.at[(0,) + slot], recv_sem=sems.at[(1,) + slot],
             device_id={"lat": dev}, device_id_type=pl.DeviceIdType.MESH)
-
-    first = []
-    for q in range(1, chips):
-        dev = lax.rem(chip + q, chips) * 2 + core
-        c = put(src, me, send.at[q], recv.at[q], dev)
         c.start()
-        first.append(c)
-    second = [put(src, me, fsend.at[0], frecv.at[0], partner)]
-    second[0].start()
-    own_block()
-    for q in range(1, chips):
-        first[q - 1].wait_recv()
-        origin = lax.rem(chip - q + chips, chips) * 2 + core
-        c = put(buf.at[origin], origin, fsend.at[q], frecv.at[q], partner)
-        c.start()
-        second.append(c)
-    for c in second:
+        started.append(c)
+        return c
+
+    along_outer, along_inner, to_partner = {}, {}, []
+    for q in range(1, outer):
+        dev = (lax.rem(z + q, outer) * inner + y) * 2 + core
+        along_outer[q] = put(src, me, outer_sem, (q,), dev)
+    for q in range(outer):
+        origin = (lax.rem(z - q + outer, outer) * inner + y) * 2 + core
+        if q:
+            along_outer[q].wait_recv()
+        block = buf.at[origin] if q else src
+        for r in range(1, inner):
+            dev = (z * inner + lax.rem(y + r, inner)) * 2 + core
+            along_inner[q, r] = put(block, origin, inner_sem, (q, r), dev)
+        to_partner.append(put(block, origin, core_sem, (q, 0), partner))
+        if q == 0:
+            own_block()
+    for q in range(outer):
+        for r in range(1, inner):
+            origin = (lax.rem(z - q + outer, outer) * inner + lax.rem(y - r + inner, inner)) * 2 + core
+            along_inner[q, r].wait_recv()
+            to_partner.append(put(buf.at[origin], origin, core_sem, (q, r), partner))
+    for c in to_partner:
         c.wait_recv()
-    return first + second
+    return started
 
 
 def forward_kernel(n, acts, enc_hbm, bias, dec_hbm, dbias,
                    xl_out, rl_out, own_out, before_out, inv_out, norm_out,
                    enc, dec, w2, xbuf, rbuf, wide, rsrc, pair_out, pair_in, sum_out, sum_in,
-                   local_sem, ag_sem, rg_sem, pair_sem, sum_sem):
+                   local_sem, pair_sem, sum_sem, *gather_sems):
+    ag_sems, rg_sems = gather_sems[:3], gather_sems[3:]
     me = lax.axis_index("lat")
     chips = n // 2
     chip, core = me // 2, me % 2
@@ -108,7 +125,7 @@
         norm_out[...] = jnp.transpose(norm)[:8, :]
         enc_copy.wait()
 
-    started = gather_kernel_body(n, acts, xbuf, weight_work, [ag_sem.at[i] for i in range(4)], me, None)
+    started = gather_blocks(n, acts, xbuf, weight_work, *ag_sems)
 
     order_rows = layer_major(rows, layers)
     before = bias[...].reshape(1, lat_dev)
@@ -165,7 +182,7 @@
     def own_residual():
         rbuf[me] = residual
 
-    started += gather_kernel_body(n, rsrc, rbuf, own_residual, [rg_sem.at[i] for i in range(4)], me, None)
+    started += gather_blocks(n, rsrc, rbuf, own_residual, *rg_sems)
     for c in range(0, width, 512):
         piece = rbuf[:, :, c:c + 512].astype(f32).reshape(rows * layers, 512).astype(bf16)
         rl_out[:, c:c + 512] = dot(order_rows, piece).astype(bf16)
@@ -173,15 +190,35 @@
         c.wait_send()
 
 
-def backward_kernel(xl, rl, own, before, inv, norm, dec, residual, genc, gencb, gdec, gdecb):
+def backward_kernel(xl, rl, own, before, inv, norm, dec_hbm, residual, genc_hbm, gencb, gdec_hbm, gdecb,
+                    dec, genc, gdec, in_sem, dec_sem, enc_sem):
     layers, width, lat_dev = genc.shape
     rows = before.shape[0]
     factor = 2.0 / rows
-    step = 512
+    pieces = dec_sem.shape[0]
+    step = width // pieces
+    cuts = [slice(i * step, (i + 1) * step) for i in range(pieces)]
+    loads = [pltpu.make_async_copy(dec_hbm.at[:, :, c], dec.at[:, :, c], in_sem.at[i]) for i, c in enumerate(cuts)]
+    for c in loads:
+        c.start()
     residual[...] = own[...].reshape(residual.shape)
+    for l in range(layers):
+        gdecb[l:l + 1, :] = factor * jnp.sum(rl[l * rows:(l + 1) * rows, :].astype(f32), axis=0, keepdims=True)
+    pre = before[...]
+    spread = spread_active(jnp.maximum(pre, 0.0).astype(bf16), layers)
+    act_sum = dot(spread, jnp.ones((rows * layers, 128), bf16), 0, 0)[:, :1]
+    scale = (sparsity_weight / rows) * act_sum * inv[...]
+    spread_t = jnp.transpose(spread)
     back = jnp.zeros((rows * layers, lat_dev * layers), f32)
-    for c in range(0, width, step):
-        back = back + dot(rl[:, c:c + step], dec[:, :, c:c + step].reshape(lat_dev * layers, step), 1, 1)
+    stores = []
+    for i, c in enumerate(cuts):
+        loads[i].wait()
+        piece = dec[:, :, c].reshape(lat_dev * layers, step)
+        back = back + dot(rl[:, c], piece, 1, 1)
+        out = factor * dot(spread_t, rl[:, c]) + scale * piece.astype(f32)
+        gdec[:, :, c] = out.astype(bf16).reshape(lat_dev, layers, step)
+        stores.append(pltpu.make_async_copy(gdec.at[:, :, c], gdec_hbm.at[:, :, c], dec_sem.at[i]))
+        stores[-1].start()
     layer = lax.broadcasted_iota(jnp.int32, (rows, lat_dev * layers), 1) % layers
     value = jnp.zeros((rows, lat_dev * layers), f32)
     for l in range(layers):
@@ -191,27 +228,22 @@
     low = (value - high.astype(f32)).astype(bf16)
     expand = pair_expander(lat_dev, layers)
     grad_act = dot(high, expand, 1, 1) + dot(low, expand, 1, 1)
-    pre = before[...]
     grad_before = jnp.where(pre > 0.0, grad_act, 0.0).astype(bf16)
     gencb[...] = jnp.sum(grad_before.astype(f32), axis=0, keepdims=True)
     for l in range(layers):
-        for c in range(0, width, step):
-            genc[l, c:c + step, :] = dot(xl[l * rows:(l + 1) * rows, c:c + step], grad_before, 0, 0).astype(bf16)
-    spread = spread_active(jnp.maximum(pre, 0.0).astype(bf16), layers)
-    act_sum = dot(spread, jnp.ones((rows * layers, 128), bf16), 0, 0)[:, :1]
-    scale = (sparsity_weight / rows) * act_sum * inv[...]
-    for c in range(0, width, step):
-        wide = dec[:, :, c:c + step].reshape(lat_dev * layers, step).astype(f32)
-        out = factor * dot(spread, rl[:, c:c + step], 0, 0) + scale * wide
-        gdec[:, :, c:c + step] = out.astype(bf16).reshape(lat_dev, layers, step)
-    for l in range(layers):
-        gdecb[l:l + 1, :] = factor * jnp.sum(rl[l * rows:(l + 1) * rows, :].astype(f32), axis=0, keepdims=True)
+        for i, c in enumerate(cuts):
+            genc[l, c, :] = dot(xl[l * rows:(l + 1) * rows, c], grad_before, 0, 0).astype(bf16)
+            stores.append(pltpu.make_async_copy(genc.at[l, c], genc_hbm.at[l, c], enc_sem.at[l, i]))
+            stores[-1].start()
+    for c in stores:
+        c.wait()
 
 
 def body(n, acts, enc_weight, enc_bias, dec_weight, dec_bias):
     tok_dev, layers, width = acts.shape
     lat_dev = enc_weight.shape[2]
     rows, block, chips = n * tok_dev, tok_dev * layers, n // 2
+    outer, inner = grid_of(n)
     vmem = pl.BlockSpec(memory_space=pltpu.VMEM)
     hbm = pl.BlockSpec(memory_space=pl.ANY)
     shape = jax.ShapeDtypeStruct
@@ -241,11 +273,9 @@
             pltpu.VMEM((chips, block, width), bf16),
             pltpu.VMEM((chips, block, width), bf16),
             dma((2,)),
-            dma((4, chips)),
-            dma((4, chips)),
             dma((2, chips)),
             dma((2, chips)),
-        ],
+        ] + [dma((2, outer)), dma((2, outer, inner)), dma((2, outer, inner))] * 2,
         compiler_params=pltpu.CompilerParams(
             collective_id=0, has_side_effects=True, vmem_limit_bytes=56 * 1024 * 1024),
         name="forward",
@@ -259,8 +289,16 @@
             shape(dec_weight.shape, bf16),
             shape(dec_bias.shape, f32),
         ),
-        in_specs=[vmem] * 7,
-        out_specs=(vmem,) * 5,
+        in_specs=[vmem] * 6 + [hbm],
+        out_specs=(vmem, hbm, vmem, hbm, vmem),
+        scratch_shapes=[
+            pltpu.VMEM(dec_weight.shape, bf16),
+            pltpu.VMEM(enc_weight.shape, bf16),
+            pltpu.VMEM(dec_weight.shape, bf16),
+            dma((4,)),
+            dma((4,)),
+            dma((layers, 4)),
+        ],
         compiler_params=pltpu.CompilerParams(vmem_limit_bytes=56 * 1024 * 1024),
         name="backward",
     )(xl, rl, own, before, inv, norm, dec_weight)

time: 42.3 us -> 44.2 us (1.045)
  Pallas kernels: 41.2 us -> 43.1 us
    pallas_call x1, Pallas kernels: 34.2 us -> 35.7 us  [body(): pl.pallas_call(functools.partial(forward_kernel, n), out_shape=(shape((ro...]
    pallas_call x1, Pallas kernels: 7 us -> 7.46 us  [body(): pl.pallas_call(backward_kernel, out_shape=(shape(acts.shape, bf16), shape...]
where the time goes in v2:
time: 44.2 us; the launch traced here: 43.8 us
  Pallas kernels  43.1 us (98%)
  between operations  0.64 us (1%)
    pallas_call x1, Pallas kernels, body(): pl.pallas_call(functools.partial(forward_kernel, n), out_shape=(shape((ro...  35.7 us
    pallas_call x1, Pallas kernels, body(): pl.pallas_call(backward_kernel, out_shape=(shape(acts.shape, bf16), shape...  7.46 us

profile of v2, /device:TPU:0, one launch (start us, length us, event | category | flops | bytes accessed | tf_op | source)
XLA Modules:
  0.0 43.8 jit_solution(6087014149909100342)
XLA Ops:
  0.6 35.7 %forward.1 = (bf16[128,2048]{1,0:T(8,128)(2,1)}, bf16[128,2048]{1,0:T(8,128)(2,1)}, bf16[8,2048]{1,0:T(8,128)(2,1)}, f32[64,256]{1,0:T(8,128)}, f32[512,1]{1,0:T(8,128)}, /*index=5*/f32[8,512]{1,0:T(8,128)}) custom-call(bf16[4,2,2048]{2,1,0:T(2,128)(2,1)} %acts.1, bf16[2,2048,256]{2,1,0:T(8,128)(2,1)} %enc_hbm.1, f32[1,256]{1,0:T(1,128)} %bitcast.2, ...), custom_call_target="tpu_custom_call" | custom-call | tf_op jit(solution)/shard_map/forward/pallas_call | solution.py:251
  36.3 7.5 %backward.1 = (bf16[4,2,2048]{2,1,0:T(2,128)(2,1)}, bf16[2,2048,256]{2,1,0:T(8,128)(2,1)}, f32[1,256]{1,0:T(1,128)}, bf16[256,2,2048]{2,1,0:T(2,128)(2,1)}, f32[2,2048]{1,0:T(2,128)}) custom-call(bf16[128,2048]{1,0:T(8,128)(2,1)} %get-tuple-element.16.xl, bf16[128,2048]{1,0:T(8,128)(2,1)} %get-tuple-element.17.rl, bf16[8,2048]{1,0:T(8,128)(2,1)} %get-tuple-element.18.own, ...), custom_call_target="tpu_custom_call" | custom-call | tf_op jit(solution)/shard_map/backward/pallas_call | solution.py:283

commit v3 on v1

--- a/solution.py
+++ b/solution.py
@@ -173,30 +173,13 @@
         c.wait_send()
 
 
-def backward_kernel(xl, rl, own, before, inv, norm, dec, residual, genc, gencb, gdec, gdecb):
+def backward_kernel(xl, rl, own, before, inv, norm, dec, residual, genc_hbm, gencb, gdec_hbm, gdecb,
+                    genc, gdec, out_sem):
     layers, width, lat_dev = genc.shape
     rows = before.shape[0]
     factor = 2.0 / rows
     step = 512
-    residual[...] = own[...].reshape(residual.shape)
-    back = jnp.zeros((rows * layers, lat_dev * layers), f32)
-    for c in range(0, width, step):
-        back = back + dot(rl[:, c:c + step], dec[:, :, c:c + step].reshape(lat_dev * layers, step), 1, 1)
-    layer = lax.broadcasted_iota(jnp.int32, (rows, lat_dev * layers), 1) % layers
-    value = jnp.zeros((rows, lat_dev * layers), f32)
-    for l in range(layers):
-        value = jnp.where(layer == l, back[l * rows:(l + 1) * rows, :], value)
-    value = factor * value + (sparsity_weight / rows) * norm[0:1, :]
-    high = value.astype(bf16)
-    low = (value - high.astype(f32)).astype(bf16)
-    expand = pair_expander(lat_dev, layers)
-    grad_act = dot(high, expand, 1, 1) + dot(low, expand, 1, 1)
     pre = before[...]
-    grad_before = jnp.where(pre > 0.0, grad_act, 0.0).astype(bf16)
-    gencb[...] = jnp.sum(grad_before.astype(f32), axis=0, keepdims=True)
-    for l in range(layers):
-        for c in range(0, width, step):
-            genc[l, c:c + step, :] = dot(xl[l * rows:(l + 1) * rows, c:c + step], grad_before, 0, 0).astype(bf16)
     spread = spread_active(jnp.maximum(pre, 0.0).astype(bf16), layers)
     act_sum = dot(spread, jnp.ones((rows * layers, 128), bf16), 0, 0)[:, :1]
     scale = (sparsity_weight / rows) * act_sum * inv[...]
@@ -204,8 +187,32 @@
         wide = dec[:, :, c:c + step].reshape(lat_dev * layers, step).astype(f32)
         out = factor * dot(spread, rl[:, c:c + step], 0, 0) + scale * wide
         gdec[:, :, c:c + step] = out.astype(bf16).reshape(lat_dev, layers, step)
+    stores = [pltpu.make_async_copy(gdec, gdec_hbm, out_sem.at[layers])]
+    stores[0].start()
+    back = jnp.zeros((rows * layers, lat_dev * layers), f32)
+    for c in range(0, width, step):
+        back = back + dot(rl[:, c:c + step], dec[:, :, c:c + step].reshape(lat_dev * layers, step), 1, 1)
+    layer = lax.broadcasted_iota(jnp.int32, (rows, lat_dev * layers), 1) % layers
+    value = jnp.zeros((rows, lat_dev * layers), f32)
+    for l in range(layers):
+        value = jnp.where(layer == l, back[l * rows:(l + 1) * rows, :], value)
+    value = factor * value + (sparsity_weight / rows) * norm[0:1, :]
+    high = value.astype(bf16)
+    low = (value - high.astype(f32)).astype(bf16)
+    expand = pair_expander(lat_dev, layers)
+    grad_act = dot(high, expand, 1, 1) + dot(low, expand, 1, 1)
+    grad_before = jnp.where(pre > 0.0, grad_act, 0.0).astype(bf16)
+    gencb[...] = jnp.sum(grad_before.astype(f32), axis=0, keepdims=True)
+    for l in range(layers):
+        for c in range(0, width, step):
+            genc[l, c:c + step, :] = dot(xl[l * rows:(l + 1) * rows, c:c + step], grad_before, 0, 0).astype(bf16)
+        stores.append(pltpu.make_async_copy(genc.at[l], genc_hbm.at[l], out_sem.at[l]))
+        stores[-1].start()
+    residual[...] = own[...].reshape(residual.shape)
     for l in range(layers):
         gdecb[l:l + 1, :] = factor * jnp.sum(rl[l * rows:(l + 1) * rows, :].astype(f32), axis=0, keepdims=True)
+    for c in stores:
+        c.wait()
 
 
 def body(n, acts, enc_weight, enc_bias, dec_weight, dec_bias):
@@ -260,7 +267,12 @@
             shape(dec_bias.shape, f32),
         ),
         in_specs=[vmem] * 7,
-        out_specs=(vmem,) * 5,
+        out_specs=(vmem, hbm, vmem, hbm, vmem),
+        scratch_shapes=[
+            pltpu.VMEM(enc_weight.shape, bf16),
+            pltpu.VMEM(dec_weight.shape, bf16),
+            dma((layers + 1,)),
+        ],
         compiler_params=pltpu.CompilerParams(vmem_limit_bytes=56 * 1024 * 1024),
         name="backward",
     )(xl, rl, own, before, inv, norm, dec_weight)

time: 42.3 us -> 42.9 us (1.014)
  Pallas kernels: 41.2 us -> 41.8 us
    pallas_call x1, Pallas kernels: 7 us -> 7.66 us  [body(): pl.pallas_call(backward_kernel, out_shape=(shape(acts.shape, bf16), shape...]
where the time goes in v3:
time: 42.9 us; the launch traced here: 42.5 us
  Pallas kernels  41.8 us (97%)
  between operations  0.64 us (1%)
    pallas_call x1, Pallas kernels, body(): pl.pallas_call(functools.partial(forward_kernel, n), out_shape=(shape((ro...  34.2 us
    pallas_call x1, Pallas kernels, body(): pl.pallas_call(backward_kernel, out_shape=(shape(acts.shape, bf16), shape...  7.66 us

profile of v3, /device:TPU:0, one launch (start us, length us, event | category | flops | bytes accessed | tf_op | source)
XLA Modules:
  0.0 42.5 jit_solution(3649624825684825394)
XLA Ops:
  0.6 34.2 %forward.1 = (bf16[128,2048]{1,0:T(8,128)(2,1)}, bf16[128,2048]{1,0:T(8,128)(2,1)}, bf16[8,2048]{1,0:T(8,128)(2,1)}, f32[64,256]{1,0:T(8,128)}, f32[512,1]{1,0:T(8,128)}, /*index=5*/f32[8,512]{1,0:T(8,128)}) custom-call(bf16[4,2,2048]{2,1,0:T(2,128)(2,1)} %acts.1, bf16[2,2048,256]{2,1,0:T(8,128)(2,1)} %enc_hbm.1, f32[1,256]{1,0:T(1,128)} %bitcast.2, ...), custom_call_target="tpu_custom_call" | custom-call | tf_op jit(solution)/shard_map/forward/pallas_call | solution.py:226
  34.8 7.7 %backward.1 = (bf16[4,2,2048]{2,1,0:T(2,128)(2,1)}, bf16[2,2048,256]{2,1,0:T(8,128)(2,1)}, f32[1,256]{1,0:T(1,128)}, bf16[256,2,2048]{2,1,0:T(2,128)(2,1)}, f32[2,2048]{1,0:T(2,128)}) custom-call(bf16[128,2048]{1,0:T(8,128)(2,1)} %get-tuple-element.16.xl, bf16[128,2048]{1,0:T(8,128)(2,1)} %get-tuple-element.17.rl, bf16[8,2048]{1,0:T(8,128)(2,1)} %get-tuple-element.18.own, ...), custom_call_target="tpu_custom_call" | custom-call | tf_op jit(solution)/shard_map/backward/pallas_call | solution.py:260

commit v4 on v1

--- a/solution.py
+++ b/solution.py
@@ -55,13 +55,13 @@
         first.append(c)
     second = [put(src, me, fsend.at[0], frecv.at[0], partner)]
     second[0].start()
-    own_block()
     for q in range(1, chips):
         first[q - 1].wait_recv()
         origin = lax.rem(chip - q + chips, chips) * 2 + core
         c = put(buf.at[origin], origin, fsend.at[q], frecv.at[q], partner)
         c.start()
         second.append(c)
+    own_block()
     for c in second:
         c.wait_recv()
     return first + second

time: 42.3 us -> 41.9 us (level)
  no operation moved by 1% of the time
where the time goes in v4:
time: 41.9 us; the launch traced here: 41.5 us
  Pallas kernels  40.8 us (97%)
  between operations  0.64 us (2%)
    pallas_call x1, Pallas kernels, body(): pl.pallas_call(functools.partial(forward_kernel, n), out_shape=(shape((ro...  33.8 us
    pallas_call x1, Pallas kernels, body(): pl.pallas_call(backward_kernel, out_shape=(shape(acts.shape, bf16), shape...  6.99 us

profile of v4, /device:TPU:0, one launch (start us, length us, event | category | flops | bytes accessed | tf_op | source)
XLA Modules:
  0.0 41.5 jit_solution(17673158019523481811)
XLA Ops:
  0.6 33.8 %forward.1 = (bf16[128,2048]{1,0:T(8,128)(2,1)}, bf16[128,2048]{1,0:T(8,128)(2,1)}, bf16[8,2048]{1,0:T(8,128)(2,1)}, f32[64,256]{1,0:T(8,128)}, f32[512,1]{1,0:T(8,128)}, /*index=5*/f32[8,512]{1,0:T(8,128)}) custom-call(bf16[4,2,2048]{2,1,0:T(2,128)(2,1)} %acts.1, bf16[2,2048,256]{2,1,0:T(8,128)(2,1)} %enc_hbm.1, f32[1,256]{1,0:T(1,128)} %bitcast.2, ...), custom_call_target="tpu_custom_call" | custom-call | tf_op jit(solution)/shard_map/forward/pallas_call | solution.py:219
  34.5 7.0 %backward.1 = (bf16[4,2,2048]{2,1,0:T(2,128)(2,1)}, bf16[2,2048,256]{2,1,0:T(8,128)(2,1)}, f32[1,256]{1,0:T(1,128)}, bf16[256,2,2048]{2,1,0:T(2,128)(2,1)}, f32[2,2048]{1,0:T(2,128)}) custom-call(bf16[128,2048]{1,0:T(8,128)(2,1)} %get-tuple-element.16.xl, bf16[128,2048]{1,0:T(8,128)(2,1)} %get-tuple-element.17.rl, bf16[8,2048]{1,0:T(8,128)(2,1)} %get-tuple-element.18.own, ...), custom_call_target="tpu_custom_call" | custom-call | tf_op jit(solution)/shard_map/backward/pallas_call | solution.py:253
